TPU v7x, 32 devices: a whole 2x2x4 slice. The times are simulated.
32 devices in a mesh: lat: 4 (over y, core), lon: 8 (over z, x).
Axes of the slice: x: 2, y: 2, z: 4, core: 2. Of those that a mesh axis runs over, the one named last changes fastest.
Arguments:
- layer_temp: float32 [64, 35, 1024], P('lat', None, 'lon'), may hold values from -20 to -2
- ice_depth_per_class: float32 [64, 5, 1024], P('lat', None, 'lon'), may hold values from 0.5 to 3
- ice_area: float32 [64, 5, 1024], P('lat', None, 'lon'), may hold values from 0.05 to 0.2
- surf_temp: float32 [64, 1024], P('lat', 'lon'), may hold values from -30 to -2
- seawater_thermal_input: float32 [64, 1024], P('lat', 'lon'), may hold values from 0 to 0.3
- velocity: float32 [2, 64, 1024], P(None, 'lat', 'lon'), may hold values from -1.2 to 1.2
- stress: float32 [3, 64, 1024], P(None, 'lat', 'lon'), may hold values from -3 to 3
- wind_stress: float32 [2, 64, 1024], P(None, 'lat', 'lon'), may hold values from -1.8 to 1.8
- current: float32 [2, 64, 1024], P(None, 'lat', 'lon'), may hold values from -1.8 to 1.8
- land_mask: int32 [64, 1024], P('lat', 'lon'), may hold values 0 or 1
- ice_mask: int32 [8, 64], P('lon', 'lat'), may hold values from 0 to 1, as said below
- band_index: int32 [64], P('lat'), may hold values from 0 to 15, as said below
Outputs:
- temp_after: float32 [64, 35, 1024], P('lat', None, 'lon')
- thick_after: float32 [64, 5, 1024], P('lat', None, 'lon')
- velocity_after: float32 [2, 64, 1024], P(None, 'lat', 'lon')
- stress_after: float32 [3, 64, 1024], P(None, 'lat', 'lon')
- zonal_volume: float32 [16], P('lat')
Inputs may be any that keep to these rules, and one draw needn't show every extreme that they name: `ice_mask`: for each lat index, the strips of all devices with that index include at most 56 ice-covered strips and more than (6) times the number of lon devices; among these devices one has all its 16 strips ice-covered. `band_index`: every band holds 1 to 7 rows, which lie next to one another; one band holds exactly 7.
All inputs are finite; a program needn't handle non-finite values. No bound on the sum of `land_mask` on one device may be relied on, other than what follows from the above.
Results may differ from a plain program's by a relative error of at most 0.00002.
Values sent between devices are 32-bit elements; how exact they have to be, the bound alone decides.
A program may use at most 64 MiB of HBM per device.

v0:
```python
import functools

import jax
import jax.numpy as jnp
from jax import lax
from jax.experimental import pallas as pl
from jax.experimental.pallas import tpu as pltpu
from jax.sharding import PartitionSpec as P

DEPTH_CLASSES = 5
VERTICAL_LEVELS = 7
SUBCYCLES = 3
SWEEPS = 2
BANDS_DEV = 4

FREEZE_POINT = -1.8
BASE_CONDUCT = 2.03
SALT_CONDUCT = 0.416
GROWTH_RATE = 0.02
STRENGTH_DECAY = 5.0
ELLIPSE_SQUARE = 4.0
STRAIN_FLOOR = 0.0025
STRESS_RELAX = 0.5
MOMENTUM_STEP = 0.5
WATER_DRAG = 1.0

HALO = 2 * SUBCYCLES
EDGE = 8
FIELDS = 10
FIRST_DYNAMIC = DEPTH_CLASSES * (VERTICAL_LEVELS + 2) + 2
DYNAMIC = 9
UNROLLED = 64

MESH = pl.DeviceIdType.MESH


def step_columns(temps, depth, surface, seawater):
    inverse = 1.0 / depth
    scaled = inverse * inverse
    half = 0.5 * scaled
    guess = temps
    for turn in range(SWEEPS):
        conduct = [BASE_CONDUCT + SALT_CONDUCT / g for g in guess]
        coupling = [scaled * conduct[0]]
        for k in range(1, VERTICAL_LEVELS):
            coupling.append(half * (conduct[k - 1] + conduct[k]))
        coupling.append(scaled * conduct[-1])
        ratio, done = [], []
        for k in range(VERTICAL_LEVELS):
            source = temps[k]
            divisor = 1.0 + coupling[k] + coupling[k + 1]
            if k == 0:
                source = source + coupling[0] * surface
            else:
                divisor = divisor - coupling[k] * ratio[k - 1]
                source = source + coupling[k] * done[k - 1]
            if k == VERTICAL_LEVELS - 1:
                source = source + coupling[k + 1] * FREEZE_POINT
            scale = 1.0 / divisor
            if k < VERTICAL_LEVELS - 1:
                ratio.append(coupling[k + 1] * scale)
            done.append(source * scale)
        solved = list(done)
        for k in range(VERTICAL_LEVELS - 2, -1, -1):
            solved[k] = done[k] + ratio[k] * solved[k + 1]
        guess = solved
    bottom = guess[-1]
    thick = (
        depth
        + GROWTH_RATE * (BASE_CONDUCT + SALT_CONDUCT / bottom) * (FREEZE_POINT - bottom) * inverse
        - seawater
    )
    return guess, thick


def subcycle(u, v, s1, s2, s12, strength, keep, push_scale, force_x, force_y):
    rows, cols = u.shape

    def dx(f):
        return pltpu.roll(f, cols - 1, 1) - pltpu.roll(f, 1, 1)

    def dy(f):
        return pltpu.roll(f, rows - 1, 0) - pltpu.roll(f, 1, 0)

    ux, vy, uy, vx = dx(u), dy(v), dy(u), dx(v)
    divergence = 0.5 * (ux + vy)
    tension = 0.5 * (ux - vy)
    shearing = 0.5 * (uy + vx)
    deformation = jnp.sqrt(
        divergence * divergence
        + (tension * tension + shearing * shearing) * (1.0 / ELLIPSE_SQUARE)
        + STRAIN_FLOOR
    )
    relax = 1.0 / (1.0 + STRESS_RELAX)
    viscous = (STRESS_RELAX * relax) * strength / deformation
    s1 = relax * s1 + viscous * (divergence - deformation)
    s2 = relax * s2 + viscous * tension * (1.0 / ELLIPSE_SQUARE)
    s12 = relax * s12 + viscous * shearing * (0.5 / ELLIPSE_SQUARE)
    push_x = dx(0.5 * (s1 + s2)) + dy(s12)
    push_y = dx(s12) + dy(0.5 * (s1 - s2))
    u = keep * u + push_scale * push_x + force_x
    v = keep * v + push_scale * push_y + force_y
    return u, v, s1, s2, s12


def as_column(row, rows):
    shape = (rows, rows)
    pick = lax.broadcasted_iota(jnp.int32, shape, 0) == lax.broadcasted_iota(jnp.int32, shape, 1)
    wide = jnp.broadcast_to(row.astype(jnp.float32), shape)
    return jnp.sum(jnp.where(pick, wide, 0.0), axis=1, keepdims=True)


def kernel(n_lat, n_lon, *refs):
    inputs, outputs, scratch = refs[:12], refs[12:17], refs[17:]
    temp_out, thick_out, vel_out, stress_out, zonal_out = outputs
    (held, land_in, ice_in, band_in, own, packed, edges, sides, parts) = scratch[:9]
    (in_sem, send_sem, recv_sem) = scratch[9:]
    rows, cols = land_in.shape
    devices = n_lat * n_lon
    lat, lon = lax.axis_index("lat"), lax.axis_index("lon")
    lats = [lax.rem(lat + d, n_lat) for d in range(n_lat)]
    lons = [lax.rem(lon + d, n_lon) for d in range(n_lon)]
    south, north, east, west = lats[1], lats[-1], lons[1], lons[-1]
    me = lon * n_lat + lat

    places = []
    first = 0
    for i in range(9):
        planes = 1 if len(inputs[i].shape) == 2 else inputs[i].shape[0]
        places.append(held.at[first] if len(inputs[i].shape) == 2 else held.at[pl.ds(first, planes)])
        first += planes
    targets = places + [land_in, ice_in, band_in]
    group = (0,) * 5 + (1,) * 4 + (2, 3, 4)

    def load(i):
        return pltpu.make_async_copy(inputs[i], targets[i], in_sem.at[group[i]])

    for i in (11, 10, 1, 2, 3, 4, 0, 5, 6, 7, 8, 9):
        load(i).start()

    def everyone(visit):
        if devices <= UNROLLED:
            for g in lons[1:] + lons[:1]:
                for a in lats:
                    if not (g is lons[0] and a is lats[0]):
                        visit((a, g))
        else:
            def step(d, carry):
                other = lax.rem(me + 1 + d, devices)
                visit((lax.rem(other, n_lat), other // n_lat))
                return carry

            lax.fori_loop(0, devices - 1, step, 0)

    barrier = pltpu.get_barrier_semaphore()
    everyone(
        lambda device: pl.semaphore_signal(
            barrier, inc=1, device_id=device, device_id_type=MESH
        )
    )

    load(11).wait()
    load(10).wait()
    icy = as_column(ice_in[...], rows) == 1.0
    width = parts.shape[-1]
    band = as_column(band_in[...], rows).astype(jnp.int32)
    slot = lax.broadcasted_iota(jnp.int32, (rows, width), 1)
    member = band == slot
    counted = jnp.where(band + width // 2 == slot, float(cols), 0.0)

    column = held.at[pl.ds(0, FIRST_DYNAMIC)]
    pltpu.make_async_copy(column, column, in_sem.at[0]).wait()
    temp_in, depth_in, area_in, surf_in, sea_in = places[:5]
    vel_in, stress_in, wind_in, current_in = places[5:]
    surface, seawater = surf_in[...], sea_in[...]
    after = jnp.zeros((rows, cols), jnp.float32)
    for c in range(DEPTH_CLASSES):
        first = c * VERTICAL_LEVELS
        temps = [temp_in[first + k] for k in range(VERTICAL_LEVELS)]
        depth = depth_in[c]
        stepped, thick = step_columns(temps, depth, surface, seawater)
        thick = jnp.where(icy, thick, depth)
        for k in range(VERTICAL_LEVELS):
            temp_out[first + k] = jnp.where(icy, stepped[k], temps[k])
        thick_out[c] = thick
        after = after + area_in[c] * thick
    total = jnp.sum(after, axis=1, keepdims=True)
    parts[pl.ds(me, 1)] = jnp.sum(jnp.where(member, total, counted), axis=0, keepdims=True)

    pl.semaphore_wait(barrier, devices - 1)

    def send_part(device):
        pltpu.make_async_remote_copy(
            src_ref=parts.at[pl.ds(me, 1)],
            dst_ref=parts.at[pl.ds(me, 1)],
            send_sem=send_sem.at[0],
            recv_sem=recv_sem.at[0],
            device_id=device,
            device_id_type=MESH,
        ).start()

    everyone(send_part)

    dynamic = held.at[pl.ds(FIRST_DYNAMIC, DYNAMIC)]
    pltpu.make_async_copy(dynamic, dynamic, in_sem.at[1]).wait()
    load(9).wait()
    volume = area_in[0] * depth_in[0]
    coverage = area_in[0]
    for c in range(1, DEPTH_CLASSES):
        volume = volume + area_in[c] * depth_in[c]
        coverage = coverage + area_in[c]
    strength = volume * jnp.exp(-STRENGTH_DECAY * (1.0 - coverage))
    drag = 1.0 / (1.0 + MOMENTUM_STEP * WATER_DRAG)
    keep = land_in[...].astype(jnp.float32) * drag
    forced = MOMENTUM_STEP * keep
    push_scale = 0.5 * forced / (1.0 + volume)
    fields = [vel_in[0], vel_in[1], stress_in[0], stress_in[1], stress_in[2], strength, keep]
    fields += [push_scale]
    fields += [forced * (wind_in[i] + WATER_DRAG * current_in[i]) for i in range(2)]
    lane = lax.broadcasted_iota(jnp.int32, (rows, cols), 1)
    pack = jnp.zeros((rows, cols), jnp.float32)
    for f in range(FIELDS):
        first = 2 * HALO * f
        turned = pltpu.roll(fields[f], (first + HALO) % cols, 1)
        pack = jnp.where((lane >= first) & (lane < first + 2 * HALO), turned, pack)
    packed[...] = pack
    for f in range(FIELDS):
        own[f] = fields[f]

    tail, head = pl.ds(rows - EDGE, EDGE), pl.ds(0, EDGE)
    above, middle, below = pl.ds(0, EDGE), pl.ds(EDGE, rows), pl.ds(EDGE + rows, EDGE)
    plan = (
        (packed.at[tail], sides.at[0, above], (south, east), 1),
        (packed.at[tail], sides.at[1, above], (south, west), 1),
        (packed.at[head], sides.at[0, below], (north, east), 1),
        (packed.at[head], sides.at[1, below], (north, west), 1),
        (packed, sides.at[0, middle], (lat, east), 1),
        (packed, sides.at[1, middle], (lat, west), 1),
        (own.at[:, tail], edges.at[0], (south, lon), 2),
        (own.at[:, head], edges.at[1], (north, lon), 2),
    )
    for source, target, device, arrival in plan:
        pltpu.make_async_remote_copy(
            src_ref=source,
            dst_ref=target,
            send_sem=send_sem.at[1],
            recv_sem=recv_sem.at[arrival],
            device_id=device,
            device_id_type=MESH,
        ).start()

    pltpu.make_async_copy(edges, edges, recv_sem.at[2]).wait()
    pltpu.make_async_copy(sides, sides, recv_sem.at[1]).wait()
    tall = rows + 2 * EDGE
    place = lax.broadcasted_iota(jnp.int32, (tall, cols), 1)
    merged = jnp.where(lax.rem(place, 2 * HALO) < HALO, sides[0], sides[1])
    low = jnp.where(lat == 0, EDGE, 0)
    high = jnp.where(lat == n_lat - 1, EDGE + rows, tall)
    row_id = lax.broadcasted_iota(jnp.int32, (tall, 2 * cols), 0)
    inside = (row_id >= low) & (row_id < high)
    state = []
    for f in range(FIELDS):
        centre = jnp.concatenate([edges[0, f], own[f], edges[1, f]], axis=0)
        beside = pltpu.roll(merged, (cols - 2 * HALO * f - HALO) % cols, 1)
        state.append(jnp.where(inside, jnp.concatenate([centre, beside], axis=1), 0.0))
    moving, fixed = state[:5], state[5:]
    for turn in range(SUBCYCLES):
        moving = subcycle(*moving, *fixed)
    for i in range(2):
        vel_out[i] = moving[i][EDGE : EDGE + rows, :cols]
    for i in range(3):
        stress_out[i] = moving[2 + i][EDGE : EDGE + rows, :cols]

    sent = held.at[pl.ds(0, (4 * EDGE + 2 * rows + 2 * FIELDS * EDGE) // rows)]
    pltpu.make_async_copy(sent, sent, send_sem.at[1]).wait()
    others = parts.at[pl.ds(0, devices - 1)]
    pltpu.make_async_copy(others, others, send_sem.at[0]).wait()
    pltpu.make_async_copy(others, others, recv_sem.at[0]).wait()
    whole = jnp.sum(parts[...], axis=0, keepdims=True)
    whole = pltpu.roll(whole, lax.rem(width - lat * BANDS_DEV, width), 1)
    cells = pltpu.roll(whole, width // 2, 1)
    mean = whole / jnp.maximum(cells, 1.0)
    zonal_out[...] = mean[:, :BANDS_DEV]


def put_out(*refs):
    sem = refs[10]
    copies = [pltpu.make_async_copy(refs[i], refs[5 + i], sem.at[i]) for i in range(5)]
    for copy in copies:
        copy.start()
    for copy in copies:
        copy.wait()


def local(n_lat, n_lon, *args):
    args = list(args)
    args[:3] = [jnp.transpose(a, (1, 0, 2)) for a in args[:3]]
    args[11] = args[11].reshape(1, -1)
    rows, cols = args[3].shape
    width = -(-2 * BANDS_DEV * n_lat // cols) * cols
    tall = rows + 2 * EDGE
    f32 = jnp.float32
    vmem = pl.BlockSpec(memory_space=pltpu.VMEM)
    shapes = [args[i].shape for i in (0, 1, 5, 6)] + [(1, BANDS_DEV)]
    dma = pltpu.SemaphoreType.DMA
    results = pl.pallas_call(
        functools.partial(kernel, n_lat, n_lon),
        out_shape=[pltpu.VMEM(shape, f32) for shape in shapes],
        in_specs=[pl.BlockSpec(memory_space=pl.ANY)] * 12,
        out_specs=[vmem] * 5,
        scratch_shapes=[
            pltpu.VMEM((FIRST_DYNAMIC + DYNAMIC, rows, cols), f32),
            *[pltpu.VMEM(a.shape, a.dtype) for a in args[9:]],
            pltpu.VMEM((FIELDS, rows, cols), f32),
            pltpu.VMEM((rows, cols), f32),
            pltpu.VMEM((2, FIELDS, EDGE, cols), f32),
            pltpu.VMEM((2, tall, cols), f32),
            pltpu.VMEM((n_lat * n_lon, width), f32),
            dma((5,)),
            dma((2,)),
            dma((3,)),
        ],
        compiler_params=pltpu.CompilerParams(collective_id=0, has_side_effects=True),
        name="ice_step",
    )(*args)
    temp, thick, vel, stress, zonal = pl.pallas_call(
        put_out,
        out_shape=[jax.ShapeDtypeStruct(shape, f32) for shape in shapes],
        in_specs=[vmem] * 5,
        out_specs=[pl.BlockSpec(memory_space=pl.ANY)] * 5,
        scratch_shapes=[dma((5,))],
        name="put_out",
    )(*[pltpu.with_memory_space_constraint(r, pltpu.VMEM) for r in results])
    temp, thick = [jnp.transpose(a, (1, 0, 2)) for a in (temp, thick)]
    return (temp, thick, vel, stress, zonal.reshape(BANDS_DEV))


def solution(mesh):
    shape = dict(mesh.shape)
    return jax.shard_map(
        functools.partial(local, shape["lat"], shape["lon"]),
        mesh=mesh,
        in_specs=(
            P("lat", None, "lon"),
            P("lat", None, "lon"),
            P("lat", None, "lon"),
            P("lat", "lon"),
            P("lat", "lon"),
            P(None, "lat", "lon"),
            P(None, "lat", "lon"),
            P(None, "lat", "lon"),
            P(None, "lat", "lon"),
            P("lat", "lon"),
            P("lon", "lat"),
            P("lat"),
        ),
        out_specs=(
            P("lat", None, "lon"),
            P("lat", None, "lon"),
            P(None, "lat", "lon"),
            P(None, "lat", "lon"),
            P("lat"),
        ),
        check_vma=False,
    )
```

profile of v0, /device:TPU:0, one launch (start us, length us, event | category | flops | bytes accessed | tf_op | source)
XLA Modules:
  0.0 12.1 jit_solution(7302572383368334243)
XLA Ops:
  0.6 10.7 %ice_step.1 = (f32[35,16,128]{2,1,0:T(8,128)S(1)}, f32[5,16,128]{2,1,0:T(8,128)S(1)}, f32[2,16,128]{2,1,0:T(8,128)S(1)}, f32[3,16,128]{2,1,0:T(8,128)S(1)}, f32[1,4]{1,0:T(1,128)S(1)}) custom-call(f32[35,16,128]{2,1,0:T(8,128)} %bitcast.7, f32[5,16,128]{2,1,0:T(8,128)} %bitcast.8, f32[5,16,128]{2,1,0:T(8,128)} %bitcast.9, f32[16,128]{1,0:T(8,128)} %refs_3_.1, ...), custom_call_target="tpu_custom_call" | custom-call | tf_op jit(solution)/shard_map/ice_step/pallas_call | solution.py:306
  11.3 0.8 %put_out.1 = (f32[35,16,128]{2,1,0:T(8,128)}, f32[5,16,128]{2,1,0:T(8,128)}, f32[2,16,128]{2,1,0:T(8,128)}, f32[3,16,128]{2,1,0:T(8,128)}, f32[1,4]{1,0:T(1,128)}) custom-call(f32[35,16,128]{2,1,0:T(8,128)S(1)} %get-tuple-element.15.refs_0_, f32[5,16,128]{2,1,0:T(8,128)S(1)} %get-tuple-element.16.refs_1_, f32[2,16,128]{2,1,0:T(8,128)S(1)} %get-tuple-element.17.refs_2_, ...), custom_call_target="tpu_custom_call" | custom-call | tf_op jit(solution)/shard_map/put_out/pallas_call | solution.py:326
where the time goes:
time: 12.3 us; the launch traced here: 12.1 us
  Pallas kernels  11.5 us (93%)
  between operations  0.64 us (5%)
    pallas_call x1, Pallas kernels, local(): pl.pallas_call(functools.partial(kernel, n_lat, n_lon), out_shape=[pltpu....  10.7 us
    pallas_call x1, Pallas kernels, local(): pl.pallas_call(put_out, out_shape=[jax.ShapeDtypeStruct(shape, f32) for s...  0.77 us

commit v1 on v0

v1 whole, which is shorter than its diff:
```python
import functools

import jax
import jax.numpy as jnp
from jax import lax
from jax.experimental import pallas as pl
from jax.experimental.pallas import tpu as pltpu
from jax.sharding import PartitionSpec as P

DEPTH_CLASSES = 5
VERTICAL_LEVELS = 7
SUBCYCLES = 3
SWEEPS = 2
BANDS_DEV = 4

FREEZE_POINT = -1.8
BASE_CONDUCT = 2.03
SALT_CONDUCT = 0.416
GROWTH_RATE = 0.02
STRENGTH_DECAY = 5.0
ELLIPSE_SQUARE = 4.0
STRAIN_FLOOR = 0.0025
STRESS_RELAX = 0.5
MOMENTUM_STEP = 0.5
WATER_DRAG = 1.0

HALO = 2 * SUBCYCLES
EDGE = 8
FIELDS = 10
COLUMN_LAYERS = DEPTH_CLASSES * VERTICAL_LEVELS
GROUPS = (2, 3)
CHUNK = 4
OUT_CHUNK = 35
UNROLLED = 64
PARTS_TURN = 2
EDGE_KINDS = ((pl.ds(0, 2), HALO), (pl.ds(2, 4), HALO - 1), (pl.ds(6, 4), HALO - 2))
EDGE_ROWS = 2 * HALO + 4 * (HALO - 1) + 4 * (HALO - 2)

MESH = pl.DeviceIdType.MESH


def step_columns(temps, depth, surface, seawater):
    inverse = 1.0 / depth
    scaled = inverse * inverse
    base, salt = BASE_CONDUCT * scaled, SALT_CONDUCT * scaled
    half = 0.5 * salt
    guess = temps
    for turn in range(SWEEPS):
        if turn > 0:
            guess = back_substitute(ratio, done)
        turned = [1.0 / g for g in guess]
        coupling = [base + salt * turned[0]]
        for k in range(1, VERTICAL_LEVELS):
            coupling.append(base + half * (turned[k - 1] + turned[k]))
        coupling.append(base + salt * turned[-1])
        pivot = 1.0 + coupling[0]
        source = temps[0] + coupling[0] * surface
        ratio, done = [], []
        for k in range(VERTICAL_LEVELS):
            if k > 0:
                pivot = 1.0 + ratio[k - 1] * pivot
                source = temps[k] + ratio[k - 1] * source
            scale = 1.0 / (pivot + coupling[k + 1])
            if k < VERTICAL_LEVELS - 1:
                ratio.append(coupling[k + 1] * scale)
            else:
                source = source + coupling[k + 1] * FREEZE_POINT
            done.append(source * scale)
    bottom = done[-1]
    thick = (
        depth
        + GROWTH_RATE * (BASE_CONDUCT + SALT_CONDUCT / bottom) * (FREEZE_POINT - bottom) * inverse
        - seawater
    )
    return ratio, done, thick


def back_substitute(ratio, done):
    solved = list(done)
    for k in range(VERTICAL_LEVELS - 2, -1, -1):
        solved[k] = done[k] + ratio[k] * solved[k + 1]
    return solved


def shift(field, beside, amount):
    cols = field.shape[1] // 2
    lane = lax.broadcasted_iota(jnp.int32, (field.shape[0], cols), 1)
    crossing = lane == (0 if amount == 1 else cols - 1)
    turned = pltpu.roll(field[:, :cols], amount % cols, 1)
    return jnp.concatenate(
        [jnp.where(crossing, beside, turned), jnp.where(crossing, turned, beside)], axis=1
    )


def subcycle(moving, fixed, beside):
    u, v, s1, s2, s12 = moving
    strength, keep, push_scale, force_x, force_y = fixed
    rows, cols = u.shape[0], u.shape[1] // 2

    def lanes(f, amount):
        return pltpu.roll(f[:, cols:], amount % cols, 1)

    def dx(f, sides=None):
        sides = sides or (lanes(f, -1), lanes(f, 1))
        return shift(f, sides[0], -1) - shift(f, sides[1], 1)

    def dy(f):
        return pltpu.roll(f, rows - 1, 0) - pltpu.roll(f, 1, 0)

    ux, vy, uy, vx = dx(u, beside[0]), dy(v), dy(u), dx(v, beside[1])
    divergence = 0.5 * (ux + vy)
    tension = 0.5 * (ux - vy)
    shearing = 0.5 * (uy + vx)
    square = (
        divergence * divergence
        + (tension * tension + shearing * shearing) * (1.0 / ELLIPSE_SQUARE)
        + STRAIN_FLOOR
    )
    inverse = lax.rsqrt(square)
    deformation = square * inverse
    relax = 1.0 / (1.0 + STRESS_RELAX)
    viscous = (STRESS_RELAX * relax) * strength * inverse
    s1 = relax * s1 + viscous * (divergence - deformation)
    s2 = relax * s2 + viscous * tension * (1.0 / ELLIPSE_SQUARE)
    s12 = relax * s12 + viscous * shearing * (0.5 / ELLIPSE_SQUARE)
    push_x = dx(0.5 * (s1 + s2)) + dy(s12)
    push_y = dx(s12) + dy(0.5 * (s1 - s2))
    u = keep * u + push_scale * push_x + force_x
    v = keep * v + push_scale * push_y + force_y
    return u, v, s1, s2, s12


def as_column(row, rows):
    shape = (rows, rows)
    pick = lax.broadcasted_iota(jnp.int32, shape, 0) == lax.broadcasted_iota(jnp.int32, shape, 1)
    wide = jnp.broadcast_to(row.astype(jnp.float32), shape)
    return jnp.sum(jnp.where(pick, wide, 0.0), axis=1, keepdims=True)


def kernel(n_lat, n_lon, *refs):
    inputs, outputs, scratch = refs[:12], refs[12:17], refs[17:]
    temp_out, thick_out, vel_out, stress_out, zonal_out = outputs
    (held, strips, land_in, own, packed, edges, sides, parts) = scratch[:8]
    (in_sem, send_sem, recv_sem) = scratch[8:]
    rows, cols = land_in.shape
    devices = n_lat * n_lon
    lat, lon = lax.axis_index("lat"), lax.axis_index("lon")
    lats = [lax.rem(lat + d, n_lat) for d in range(n_lat)]
    lons = [lax.rem(lon + d, n_lon) for d in range(n_lon)]
    south, north, east, west = lats[1], lats[-1], lons[1], lons[-1]
    me = lon * n_lat + lat
    at_top, at_bottom = lat == 0, lat == n_lat - 1
    at_rim = at_top | at_bottom

    (temp_src, depth_src, area_src, surf_src, sea_src, vel_src, stress_src) = inputs[:7]
    (wind_src, current_src, land_src, ice_src, band_src) = inputs[7:]
    surf_in, sea_in = held.at[0], held.at[1]
    depth_at = range(2, 2 + DEPTH_CLASSES)
    area_at = range(2 + DEPTH_CLASSES, 2 + 2 * DEPTH_CLASSES)
    first_temp = 2 + 2 * DEPTH_CLASSES
    temp_at = range(first_temp, first_temp + COLUMN_LAYERS)
    temp_loads, blocks = [], []
    layer = 0
    for group, count in enumerate(GROUPS):
        end = layer + count * VERTICAL_LEVELS
        begin = first_temp + layer if group else 0
        blocks.append(held.at[pl.ds(begin, first_temp + end - begin)])
        temp_loads.append([])
        while layer < end:
            some = min(CHUNK, end - layer)
            temp_loads[group].append(
                (temp_src.at[pl.ds(layer, some)], held.at[pl.ds(first_temp + layer, some)], group)
            )
            layer += some
    start = first_temp + COLUMN_LAYERS
    last = len(GROUPS) - 1
    vel_in, stress_in = held.at[pl.ds(start, 2)], held.at[pl.ds(start + 2, 3)]
    wind_in, current_in = held.at[pl.ds(start + 5, 2)], held.at[pl.ds(start + 7, 2)]
    fast_loads = [
        (vel_src, vel_in, last + 3),
        (stress_src, stress_in, last + 3),
        (wind_src, wind_in, last + 3),
        (current_src, current_in, last + 3),
        (land_src, land_in, last + 2),
    ]
    loads = [
        (surf_src, surf_in, 0),
        (sea_src, sea_in, 0),
        (depth_src, held.at[pl.ds(2, DEPTH_CLASSES)], 0),
        *temp_loads[0],
        (area_src, held.at[pl.ds(2 + DEPTH_CLASSES, DEPTH_CLASSES)], 0),
        (band_src, strips.at[0], last + 1),
        (ice_src, strips.at[1], last + 1),
        *fast_loads,
        *[load for group in temp_loads[1:] for load in group],
    ]
    for source, target, group in loads:
        pltpu.make_async_copy(source, target, in_sem.at[group]).start()

    def arrive(ref, semaphore):
        pltpu.make_async_copy(ref, ref, semaphore).wait()

    def arrive_planes(inner, rim, semaphore):
        @pl.when(at_rim)
        def _():
            arrive(held.at[pl.ds(0, rim)], semaphore)

        @pl.when(jnp.logical_not(at_rim))
        def _():
            arrive(held.at[pl.ds(0, inner)], semaphore)

    pairs = [(a, g) for g in lons[1:] for a in lats] + [(a, lon) for a in lats[1:]]

    def everyone(visit):
        def step(d, carry):
            other = lax.rem(me + 1 + d, devices)
            visit((lax.rem(other, n_lat), other // n_lat))
            return carry

        lax.fori_loop(0, devices - 1, step, 0)

    barrier = pltpu.get_barrier_semaphore()

    def greet(device):
        pl.semaphore_signal(barrier, inc=1, device_id=device, device_id_type=MESH)

    if devices <= UNROLLED:
        for pair in pairs[1 - n_lat :] + pairs[: 1 - n_lat]:
            greet(pair)
    else:
        everyone(greet)

    kept = []

    def thermo(c):
        temps = [held[temp_at[c * VERTICAL_LEVELS + k]] for k in range(VERTICAL_LEVELS)]
        depth = held[depth_at[c]]
        ratio, done, thick = step_columns(temps, depth, surf_in[...], sea_in[...])
        kept.append((ratio, done, thick))

    def finish_temps(c):
        for k, solved in enumerate(back_substitute(*kept[c][:2])):
            temp = held[temp_at[c * VERTICAL_LEVELS + k]]
            temp_out[c * VERTICAL_LEVELS + k] = jnp.where(icy, solved, temp)

    def send_part(device):
        pltpu.make_async_remote_copy(
            src_ref=parts.at[pl.ds(me, 1)],
            dst_ref=parts.at[pl.ds(me, 1)],
            send_sem=send_sem.at[0],
            recv_sem=recv_sem.at[0],
            device_id=device,
            device_id_type=MESH,
        ).start()

    def send_halo(source, target, device, arrival):
        pltpu.make_async_remote_copy(
            src_ref=source,
            dst_ref=target,
            send_sem=send_sem.at[1],
            recv_sem=recv_sem.at[arrival],
            device_id=device,
            device_id_type=MESH,
        ).start()

    arrive(blocks[0], in_sem.at[0])
    for c in range(0, 2):
        thermo(c)
    arrive(blocks[1], in_sem.at[1])
    arrive(held.at[pl.ds(start, 9)], in_sem.at[last + 3])
    arrive(land_in, in_sem.at[last + 2])
    arrive(strips, in_sem.at[last + 1])
    icy = as_column(strips[1], rows) == 1.0
    width = parts.shape[-1]
    band = as_column(strips[0], rows).astype(jnp.int32)
    slot = lax.broadcasted_iota(jnp.int32, (rows, width), 1)
    member = band == slot
    counted = jnp.where(band + width // 2 == slot, float(cols), 0.0)

    for c in range(2, 5):
        thermo(c)
    volume = held[area_at[0]] * held[depth_at[0]]
    coverage = held[area_at[0]]
    for c in range(1, DEPTH_CLASSES):
        volume = volume + held[area_at[c]] * held[depth_at[c]]
        coverage = coverage + held[area_at[c]]
    strength = volume * jnp.exp(-STRENGTH_DECAY * (1.0 - coverage))
    drag = 1.0 / (1.0 + MOMENTUM_STEP * WATER_DRAG)
    keep = land_in[...].astype(jnp.float32) * drag
    forced = MOMENTUM_STEP * keep
    push_scale = 0.5 * forced / (1.0 + volume)
    fields = [vel_in[0], vel_in[1], stress_in[0], stress_in[1], stress_in[2], strength, keep]
    fields += [push_scale]
    fields += [forced * (wind_in[i] + WATER_DRAG * current_in[i]) for i in range(2)]
    lane = lax.broadcasted_iota(jnp.int32, (rows, cols), 1)
    pack = jnp.zeros((rows, cols), jnp.float32)
    for f in range(FIELDS):
        first = 2 * HALO * f
        turned = pltpu.roll(fields[f], (first + HALO) % cols, 1)
        pack = jnp.where((lane >= first) & (lane < first + 2 * HALO), turned, pack)
    packed[...] = pack
    for f in range(FIELDS):
        own[f] = fields[f]

    after = jnp.zeros((rows, cols), jnp.float32)
    for c in range(DEPTH_CLASSES):
        thick = jnp.where(icy, kept[c][2], held[depth_at[c]])
        thick_out[c] = thick
        after = after + held[area_at[c]] * thick
    total = jnp.sum(after, axis=1, keepdims=True)
    parts[pl.ds(me, 1)] = jnp.sum(jnp.where(member, total, counted), axis=0, keepdims=True)
    pl.semaphore_wait(barrier, devices - 1)

    if devices <= UNROLLED:
        for pair in pairs[0:4]:
            send_part(pair)

    tail, head = pl.ds(rows - EDGE, EDGE), pl.ds(0, EDGE)
    above, middle, below = pl.ds(0, EDGE), pl.ds(EDGE, rows), pl.ds(EDGE + rows, EDGE)
    send_halo(packed, sides.at[0, middle], (lat, east), 1)
    send_halo(packed, sides.at[1, middle], (lat, west), 1)

    @pl.when(jnp.logical_not(at_bottom))
    def _():
        send_halo(packed.at[tail], sides.at[0, above], (south, east), 1)
        send_halo(packed.at[tail], sides.at[1, above], (south, west), 1)
        for kind, reach in EDGE_KINDS:
            send_halo(
                own.at[kind, pl.ds(rows - reach, reach)],
                edges.at[0, kind, pl.ds(EDGE - reach, reach)],
                (south, lon),
                2,
            )

    @pl.when(jnp.logical_not(at_top))
    def _():
        send_halo(packed.at[head], sides.at[0, below], (north, east), 1)
        send_halo(packed.at[head], sides.at[1, below], (north, west), 1)
        for kind, reach in EDGE_KINDS:
            send_halo(
                own.at[kind, pl.ds(0, reach)],
                edges.at[1, kind, pl.ds(0, reach)],
                (north, lon),
                2,
            )

    if devices <= UNROLLED:
        for pair in pairs[4:]:
            send_part(pair)
    else:
        everyone(send_part)

    for c in range(DEPTH_CLASSES):
        finish_temps(c)

    def finish_zonal():
        whole = jnp.sum(parts[...], axis=0, keepdims=True)
        whole = pltpu.roll(whole, lax.rem(width - lat * BANDS_DEV, width), 1)
        cells = pltpu.roll(whole, width // 2, 1)
        mean = whole / jnp.maximum(cells, 1.0)
        zonal_out[...] = mean[:, :BANDS_DEV]

    brim = EDGE_ROWS // rows
    arrive_planes(2 * brim, brim, recv_sem.at[2])
    arrive_planes(4, 3, recv_sem.at[1])
    tall = rows + 2 * EDGE
    low = jnp.where(at_top, EDGE, 0)
    high = jnp.where(at_bottom, EDGE + rows, tall)
    row_id = lax.broadcasted_iota(jnp.int32, (tall, cols), 0)
    inside = (row_id >= low) & (row_id < high)
    place = lax.broadcasted_iota(jnp.int32, (tall, cols), 1)
    merged = jnp.where(lax.rem(place, 2 * HALO) < HALO, sides[0], sides[1])
    merged = jnp.where(inside, merged, 0.0)

    def beside(f, amount):
        return pltpu.roll(merged, (2 * cols - 2 * HALO * f - HALO + amount) % cols, 1)

    state = []
    for f in range(FIELDS):
        centre = jnp.concatenate([edges[0, f], own[f], edges[1, f]], axis=0)
        centre = jnp.where(inside, centre, 0.0)
        state.append(jnp.concatenate([centre, beside(f, 0)], axis=1))
    moving, fixed = state[:5], state[5:]
    first_beside = [(beside(f, -1), beside(f, 1)) for f in range(2)]
    others = parts.at[pl.ds(0, devices - 1)]
    for turn in range(SUBCYCLES):
        if turn == PARTS_TURN:
            arrive(others, recv_sem.at[0])
            finish_zonal()
        moving = subcycle(moving, fixed, first_beside if turn == 0 else (None, None))
    for i in range(2):
        vel_out[i] = moving[i][EDGE : EDGE + rows, :cols]
    for i in range(3):
        stress_out[i] = moving[2 + i][EDGE : EDGE + rows, :cols]

    if PARTS_TURN == SUBCYCLES:
        arrive(others, recv_sem.at[0])
        finish_zonal()
    arrive_planes(2 + 2 * (brim + 1), 2 + brim + 1, send_sem.at[1])
    arrive(others, send_sem.at[0])


def put_out(temp, thick, vel, stress, zonal, *refs):
    outs, sem = refs[:5], refs[5]
    planes = [ref.shape[0] for ref in (thick, vel, stress)]
    copies = [(zonal, outs[4], 2), (vel, outs[2], 1), (stress, outs[3], 1), (thick, outs[1], 1)]
    for first in range(0, COLUMN_LAYERS, OUT_CHUNK):
        some = pl.ds(first, min(OUT_CHUNK, COLUMN_LAYERS - first))
        copies.append((temp.at[some], outs[0].at[some], 0))
    for source, target, group in copies:
        pltpu.make_async_copy(source, target, sem.at[group]).start()
    pltpu.make_async_copy(temp, outs[0], sem.at[0]).wait()
    small = pl.ds(0, sum(planes))
    pltpu.make_async_copy(temp.at[small], outs[0].at[small], sem.at[1]).wait()
    pltpu.make_async_copy(zonal, outs[4], sem.at[2]).wait()


def local(n_lat, n_lon, *args):
    args = list(args)
    args[:3] = [jnp.transpose(a, (1, 0, 2)) for a in args[:3]]
    args[11] = args[11].reshape(1, -1)
    rows, cols = args[3].shape
    width = -(-2 * BANDS_DEV * n_lat // cols) * cols
    tall = rows + 2 * EDGE
    f32 = jnp.float32
    vmem = pl.BlockSpec(memory_space=pltpu.VMEM)
    shapes = [args[i].shape for i in (0, 1, 5, 6)] + [(1, BANDS_DEV)]
    dma = pltpu.SemaphoreType.DMA
    results = pl.pallas_call(
        functools.partial(kernel, n_lat, n_lon),
        out_shape=[pltpu.VMEM(shape, f32) for shape in shapes],
        in_specs=[pl.BlockSpec(memory_space=pl.ANY)] * 12,
        out_specs=[vmem] * 5,
        scratch_shapes=[
            pltpu.VMEM((2 * DEPTH_CLASSES + 2 + COLUMN_LAYERS + 9, rows, cols), f32),
            pltpu.VMEM((2, 1, rows), jnp.int32),
            pltpu.VMEM((rows, cols), jnp.int32),
            pltpu.VMEM((FIELDS, rows, cols), f32),
            pltpu.VMEM((rows, cols), f32),
            pltpu.VMEM((2, FIELDS, EDGE, cols), f32),
            pltpu.VMEM((2, tall, cols), f32),
            pltpu.VMEM((n_lat * n_lon, width), f32),
            dma((len(GROUPS) + 3,)),
            dma((2,)),
            dma((3,)),
        ],
        compiler_params=pltpu.CompilerParams(collective_id=0, has_side_effects=True),
        name="ice_step",
    )(*args)
    temp, thick, vel, stress, zonal = pl.pallas_call(
        put_out,
        out_shape=[jax.ShapeDtypeStruct(shape, f32) for shape in shapes],
        in_specs=[vmem] * 5,
        out_specs=[pl.BlockSpec(memory_space=pl.ANY)] * 5,
        scratch_shapes=[dma((3,))],
        name="put_out",
    )(*[pltpu.with_memory_space_constraint(r, pltpu.VMEM) for r in results])
    temp, thick = [jnp.transpose(a, (1, 0, 2)) for a in (temp, thick)]
    return (temp, thick, vel, stress, zonal.reshape(BANDS_DEV))


def solution(mesh):
    shape = dict(mesh.shape)
    return jax.shard_map(
        functools.partial(local, shape["lat"], shape["lon"]),
        mesh=mesh,
        in_specs=(
            P("lat", None, "lon"),
            P("lat", None, "lon"),
            P("lat", None, "lon"),
            P("lat", "lon"),
            P("lat", "lon"),
            P(None, "lat", "lon"),
            P(None, "lat", "lon"),
            P(None, "lat", "lon"),
            P(None, "lat", "lon"),
            P("lat", "lon"),
            P("lon", "lat"),
            P("lat"),
        ),
        out_specs=(
            P("lat", None, "lon"),
            P("lat", None, "lon"),
            P(None, "lat", "lon"),
            P(None, "lat", "lon"),
            P("lat"),
        ),
        check_vma=False,
    )
```

time: 12.3 us -> 12 us (0.976)
  the two profiles are of different devices: /device:TPU:0 before, /device:TPU:1 now
where the time goes in v1:
time: 12 us; the launch traced here: 11.8 us
  Pallas kernels  11.1 us (92%)
  between operations  0.64 us (5%)
    pallas_call x1, Pallas kernels, local(): pl.pallas_call(functools.partial(kernel, n_lat, n_lon), out_shape=[pltpu....  10.4 us
    pallas_call x1, Pallas kernels, local(): pl.pallas_call(put_out, out_shape=[jax.ShapeDtypeStruct(shape, f32) for s...  0.77 us

profile of v1, /device:TPU:1, one launch (start us, length us, event | category | flops | bytes accessed | tf_op | source)
XLA Modules:
  0.0 11.8 jit_solution(8062880629852809396)
XLA Ops:
  0.6 10.4 %ice_step.1 = (f32[35,16,128]{2,1,0:T(8,128)S(1)}, f32[5,16,128]{2,1,0:T(8,128)S(1)}, f32[2,16,128]{2,1,0:T(8,128)S(1)}, f32[3,16,128]{2,1,0:T(8,128)S(1)}, f32[1,4]{1,0:T(1,128)S(1)}) custom-call(f32[35,16,128]{2,1,0:T(8,128)} %bitcast.7, f32[5,16,128]{2,1,0:T(8,128)} %bitcast.8, f32[5,16,128]{2,1,0:T(8,128)} %bitcast.9, f32[16,128]{1,0:T(8,128)} %refs_3_.1, ...), custom_call_target="tpu_custom_call" | custom-call | tf_op jit(solution)/shard_map/ice_step/pallas_call | solution.py:429
  11.0 0.8 %put_out.1 = (f32[35,16,128]{2,1,0:T(8,128)}, f32[5,16,128]{2,1,0:T(8,128)}, f32[2,16,128]{2,1,0:T(8,128)}, f32[3,16,128]{2,1,0:T(8,128)}, f32[1,4]{1,0:T(1,128)}) custom-call(f32[35,16,128]{2,1,0:T(8,128)S(1)} %get-tuple-element.15.temp, f32[5,16,128]{2,1,0:T(8,128)S(1)} %get-tuple-element.16.thick, f32[2,16,128]{2,1,0:T(8,128)S(1)} %get-tuple-element.17.vel, ...), custom_call_target="tpu_custom_call" | custom-call | tf_op jit(solution)/shard_map/put_out/pallas_call | solution.py:450

commit v2 on v1

--- a/solution.py
+++ b/solution.py
@@ -29,10 +29,11 @@
 FIELDS = 10
 COLUMN_LAYERS = DEPTH_CLASSES * VERTICAL_LEVELS
 GROUPS = (2, 3)
+FAST = 2 * DEPTH_CLASSES + 9
 CHUNK = 4
-OUT_CHUNK = 35
+OUT_CHUNK = 4
 UNROLLED = 64
-PARTS_TURN = 2
+PARTS_TURN = 3
 EDGE_KINDS = ((pl.ds(0, 2), HALO), (pl.ds(2, 4), HALO - 1), (pl.ds(6, 4), HALO - 2))
 EDGE_ROWS = 2 * HALO + 4 * (HALO - 1) + 4 * (HALO - 2)
 
@@ -140,8 +141,8 @@
 def kernel(n_lat, n_lon, *refs):
     inputs, outputs, scratch = refs[:12], refs[12:17], refs[17:]
     temp_out, thick_out, vel_out, stress_out, zonal_out = outputs
-    (held, strips, land_in, own, packed, edges, sides, parts) = scratch[:8]
-    (in_sem, send_sem, recv_sem) = scratch[8:]
+    (held, strips, land_in, own, packed, edges, sides, parts, outbox) = scratch[:9]
+    (in_sem, send_sem, recv_sem) = scratch[9:]
     rows, cols = land_in.shape
     devices = n_lat * n_lon
     lat, lon = lax.axis_index("lat"), lax.axis_index("lon")
@@ -154,16 +155,16 @@
 
     (temp_src, depth_src, area_src, surf_src, sea_src, vel_src, stress_src) = inputs[:7]
     (wind_src, current_src, land_src, ice_src, band_src) = inputs[7:]
-    surf_in, sea_in = held.at[0], held.at[1]
-    depth_at = range(2, 2 + DEPTH_CLASSES)
-    area_at = range(2 + DEPTH_CLASSES, 2 + 2 * DEPTH_CLASSES)
-    first_temp = 2 + 2 * DEPTH_CLASSES
+    surf_in, sea_in = held.at[FAST], held.at[FAST + 1]
+    depth_at = range(DEPTH_CLASSES)
+    area_at = range(DEPTH_CLASSES, 2 * DEPTH_CLASSES)
+    first_temp = FAST + 2
     temp_at = range(first_temp, first_temp + COLUMN_LAYERS)
     temp_loads, blocks = [], []
     layer = 0
     for group, count in enumerate(GROUPS):
         end = layer + count * VERTICAL_LEVELS
-        begin = first_temp + layer if group else 0
+        begin = first_temp + layer if group else FAST
         blocks.append(held.at[pl.ds(begin, first_temp + end - begin)])
         temp_loads.append([])
         while layer < end:
@@ -172,7 +173,7 @@
                 (temp_src.at[pl.ds(layer, some)], held.at[pl.ds(first_temp + layer, some)], group)
             )
             layer += some
-    start = first_temp + COLUMN_LAYERS
+    start = 2 * DEPTH_CLASSES
     last = len(GROUPS) - 1
     vel_in, stress_in = held.at[pl.ds(start, 2)], held.at[pl.ds(start + 2, 3)]
     wind_in, current_in = held.at[pl.ds(start + 5, 2)], held.at[pl.ds(start + 7, 2)]
@@ -184,14 +185,14 @@
         (land_src, land_in, last + 2),
     ]
     loads = [
+        *fast_loads,
+        (depth_src, held.at[pl.ds(0, DEPTH_CLASSES)], last + 3),
+        (area_src, held.at[pl.ds(DEPTH_CLASSES, DEPTH_CLASSES)], last + 3),
         (surf_src, surf_in, 0),
         (sea_src, sea_in, 0),
-        (depth_src, held.at[pl.ds(2, DEPTH_CLASSES)], 0),
         *temp_loads[0],
-        (area_src, held.at[pl.ds(2 + DEPTH_CLASSES, DEPTH_CLASSES)], 0),
         (band_src, strips.at[0], last + 1),
         (ice_src, strips.at[1], last + 1),
-        *fast_loads,
         *[load for group in temp_loads[1:] for load in group],
     ]
     for source, target, group in loads:
@@ -209,7 +210,7 @@
         def _():
             arrive(held.at[pl.ds(0, inner)], semaphore)
 
-    pairs = [(a, g) for g in lons[1:] for a in lats] + [(a, lon) for a in lats[1:]]
+    pairs = [(a, g) for g in lons[1:] for a in lats[n_lat // 2 :] + lats[: n_lat // 2]] + [(a, lon) for a in lats[1:]]
 
     def everyone(visit):
         def step(d, carry):
@@ -245,8 +246,8 @@
 
     def send_part(device):
         pltpu.make_async_remote_copy(
-            src_ref=parts.at[pl.ds(me, 1)],
-            dst_ref=parts.at[pl.ds(me, 1)],
+            src_ref=outbox.at[pl.ds(2 * device[0], 2)],
+            dst_ref=parts.at[pl.ds(2 * me, 2)],
             send_sem=send_sem.at[0],
             recv_sem=recv_sem.at[0],
             device_id=device,
@@ -263,22 +264,9 @@
             device_id_type=MESH,
         ).start()
 
+    arrive(held.at[pl.ds(0, FAST)], in_sem.at[last + 3])
+    arrive(land_in, in_sem.at[last + 2])
     arrive(blocks[0], in_sem.at[0])
-    for c in range(0, 2):
-        thermo(c)
-    arrive(blocks[1], in_sem.at[1])
-    arrive(held.at[pl.ds(start, 9)], in_sem.at[last + 3])
-    arrive(land_in, in_sem.at[last + 2])
-    arrive(strips, in_sem.at[last + 1])
-    icy = as_column(strips[1], rows) == 1.0
-    width = parts.shape[-1]
-    band = as_column(strips[0], rows).astype(jnp.int32)
-    slot = lax.broadcasted_iota(jnp.int32, (rows, width), 1)
-    member = band == slot
-    counted = jnp.where(band + width // 2 == slot, float(cols), 0.0)
-
-    for c in range(2, 5):
-        thermo(c)
     volume = held[area_at[0]] * held[depth_at[0]]
     coverage = held[area_at[0]]
     for c in range(1, DEPTH_CLASSES):
@@ -302,18 +290,9 @@
     for f in range(FIELDS):
         own[f] = fields[f]
 
-    after = jnp.zeros((rows, cols), jnp.float32)
-    for c in range(DEPTH_CLASSES):
-        thick = jnp.where(icy, kept[c][2], held[depth_at[c]])
-        thick_out[c] = thick
-        after = after + held[area_at[c]] * thick
-    total = jnp.sum(after, axis=1, keepdims=True)
-    parts[pl.ds(me, 1)] = jnp.sum(jnp.where(member, total, counted), axis=0, keepdims=True)
+    for c in range(0, 2):
+        thermo(c)
     pl.semaphore_wait(barrier, devices - 1)
-
-    if devices <= UNROLLED:
-        for pair in pairs[0:4]:
-            send_part(pair)
 
     tail, head = pl.ds(rows - EDGE, EDGE), pl.ds(0, EDGE)
     above, middle, below = pl.ds(0, EDGE), pl.ds(EDGE, rows), pl.ds(EDGE + rows, EDGE)
@@ -344,8 +323,29 @@
                 2,
             )
 
+    arrive(blocks[1], in_sem.at[1])
+    arrive(strips, in_sem.at[last + 1])
+    icy = as_column(strips[1], rows) == 1.0
+    band = as_column(strips[0], rows).astype(jnp.int32)
+    slot = lax.broadcasted_iota(jnp.int32, (rows, cols), 1)
+    slot = jnp.where(slot < BANDS_DEV, slot, -BANDS_DEV * n_lat)
+    members = [band - BANDS_DEV * a == slot for a in range(n_lat)]
+    for a in range(n_lat):
+        counted = jnp.where(members[a], float(cols), 0.0)
+        outbox[pl.ds(2 * a + 1, 1)] = jnp.sum(counted, axis=0, keepdims=True)
+
+    for c in range(2, 5):
+        thermo(c)
+    after = jnp.zeros((rows, cols), jnp.float32)
+    for c in range(DEPTH_CLASSES):
+        thick = jnp.where(icy, kept[c][2], held[depth_at[c]])
+        thick_out[c] = thick
+        after = after + held[area_at[c]] * thick
+    total = jnp.sum(after, axis=1, keepdims=True)
+    for a in range(n_lat):
+        outbox[pl.ds(2 * a, 1)] = jnp.sum(jnp.where(members[a], total, 0.0), axis=0, keepdims=True)
     if devices <= UNROLLED:
-        for pair in pairs[4:]:
+        for pair in pairs[0:]:
             send_part(pair)
     else:
         everyone(send_part)
@@ -353,11 +353,13 @@
     for c in range(DEPTH_CLASSES):
         finish_temps(c)
 
+    parts[pl.ds(2 * me, 2)] = outbox[pl.ds(2 * lat, 2)]
+
     def finish_zonal():
-        whole = jnp.sum(parts[...], axis=0, keepdims=True)
-        whole = pltpu.roll(whole, lax.rem(width - lat * BANDS_DEV, width), 1)
-        cells = pltpu.roll(whole, width // 2, 1)
-        mean = whole / jnp.maximum(cells, 1.0)
+        whole = jnp.sum(parts[...].reshape(-1, 8, cols), axis=0)
+        whole = whole + pltpu.roll(whole, 4, 0)
+        whole = whole + pltpu.roll(whole, 2, 0)
+        mean = whole[:1] / jnp.maximum(whole[1:2], 1.0)
         zonal_out[...] = mean[:, :BANDS_DEV]
 
     brim = EDGE_ROWS // rows
@@ -382,7 +384,7 @@
         state.append(jnp.concatenate([centre, beside(f, 0)], axis=1))
     moving, fixed = state[:5], state[5:]
     first_beside = [(beside(f, -1), beside(f, 1)) for f in range(2)]
-    others = parts.at[pl.ds(0, devices - 1)]
+    others = parts.at[pl.ds(0, 2 * (devices - 1))]
     for turn in range(SUBCYCLES):
         if turn == PARTS_TURN:
             arrive(others, recv_sem.at[0])
@@ -393,11 +395,11 @@
     for i in range(3):
         stress_out[i] = moving[2 + i][EDGE : EDGE + rows, :cols]
 
+    arrive_planes(2 + 2 * (brim + 1), 2 + brim + 1, send_sem.at[1])
+    arrive(others, send_sem.at[0])
     if PARTS_TURN == SUBCYCLES:
         arrive(others, recv_sem.at[0])
         finish_zonal()
-    arrive_planes(2 + 2 * (brim + 1), 2 + brim + 1, send_sem.at[1])
-    arrive(others, send_sem.at[0])
 
 
 def put_out(temp, thick, vel, stress, zonal, *refs):
@@ -420,7 +422,6 @@
     args[:3] = [jnp.transpose(a, (1, 0, 2)) for a in args[:3]]
     args[11] = args[11].reshape(1, -1)
     rows, cols = args[3].shape
-    width = -(-2 * BANDS_DEV * n_lat // cols) * cols
     tall = rows + 2 * EDGE
     f32 = jnp.float32
     vmem = pl.BlockSpec(memory_space=pltpu.VMEM)
@@ -439,7 +440,8 @@
             pltpu.VMEM((rows, cols), f32),
             pltpu.VMEM((2, FIELDS, EDGE, cols), f32),
             pltpu.VMEM((2, tall, cols), f32),
-            pltpu.VMEM((n_lat * n_lon, width), f32),
+            pltpu.VMEM((2 * n_lat * n_lon, cols), f32),
+            pltpu.VMEM((2 * n_lat, cols), f32),
             dma((len(GROUPS) + 3,)),
             dma((2,)),
             dma((3,)),

time: 12 us -> 11.8 us (0.983)
  the two profiles are of different devices: /device:TPU:1 before, /device:TPU:0 now
where the time goes in v2:
time: 11.8 us; the launch traced here: 11.6 us
  Pallas kernels  11 us (93%)
  between operations  0.64 us (5%)
    pallas_call x1, Pallas kernels, local(): pl.pallas_call(functools.partial(kernel, n_lat, n_lon), out_shape=[pltpu....  10.2 us
    pallas_call x1, Pallas kernels, local(): pl.pallas_call(put_out, out_shape=[jax.ShapeDtypeStruct(shape, f32) for s...  0.75 us

profile of v2, /device:TPU:0, one launch (start us, length us, event | category | flops | bytes accessed | tf_op | source)
XLA Modules:
  0.0 11.6 jit_solution(58274830386784537)
XLA Ops:
  0.6 10.2 %ice_step.1 = (f32[35,16,128]{2,1,0:T(8,128)S(1)}, f32[5,16,128]{2,1,0:T(8,128)S(1)}, f32[2,16,128]{2,1,0:T(8,128)S(1)}, f32[3,16,128]{2,1,0:T(8,128)S(1)}, f32[1,4]{1,0:T(1,128)S(1)}) custom-call(f32[35,16,128]{2,1,0:T(8,128)} %bitcast.7, f32[5,16,128]{2,1,0:T(8,128)} %bitcast.8, f32[5,16,128]{2,1,0:T(8,128)} %bitcast.9, f32[16,128]{1,0:T(8,128)} %refs_3_.1, ...), custom_call_target="tpu_custom_call" | custom-call | tf_op jit(solution)/shard_map/ice_step/pallas_call | solution.py:430
  10.8 0.8 %put_out.1 = (f32[35,16,128]{2,1,0:T(8,128)}, f32[5,16,128]{2,1,0:T(8,128)}, f32[2,16,128]{2,1,0:T(8,128)}, f32[3,16,128]{2,1,0:T(8,128)}, f32[1,4]{1,0:T(1,128)}) custom-call(f32[35,16,128]{2,1,0:T(8,128)S(1)} %get-tuple-element.15.temp, f32[5,16,128]{2,1,0:T(8,128)S(1)} %get-tuple-element.16.thick, f32[2,16,128]{2,1,0:T(8,128)S(1)} %get-tuple-element.17.vel, ...), custom_call_target="tpu_custom_call" | custom-call | tf_op jit(solution)/shard_map/put_out/pallas_call | solution.py:452

commit v3 on v2

--- a/solution.py
+++ b/solution.py
@@ -34,10 +34,39 @@
 OUT_CHUNK = 4
 UNROLLED = 64
 PARTS_TURN = 3
-EDGE_KINDS = ((pl.ds(0, 2), HALO), (pl.ds(2, 4), HALO - 1), (pl.ds(6, 4), HALO - 2))
-EDGE_ROWS = 2 * HALO + 4 * (HALO - 1) + 4 * (HALO - 2)
+EDGE_KINDS = ((pl.ds(0, 6), HALO), (pl.ds(6, 4), HALO + 1))
+EDGE_ROWS = 6 * HALO + 4 * (HALO + 1)
 
 MESH = pl.DeviceIdType.MESH
+
+
+def eliminate(temps, outside, coupling):
+    pivot = 1.0 + coupling[0]
+    source = temps[0] + coupling[0] * outside
+    ratio, done = [], []
+    for k in range(1, len(temps)):
+        scale = 1.0 / (pivot + coupling[k])
+        ratio.append(coupling[k] * scale)
+        done.append(source * scale)
+        pivot = 1.0 + ratio[-1] * pivot
+        source = temps[k] + ratio[-1] * source
+    return ratio, done, pivot, source
+
+
+def meet(temps, surface, coupling):
+    mid = VERTICAL_LEVELS // 2
+    upper, above, pivot, source = eliminate(temps[: mid + 1], surface, coupling)
+    lower, below, pivot_low, source_low = eliminate(temps[:mid:-1], FREEZE_POINT, coupling[::-1])
+    scale = 1.0 / (pivot_low + coupling[mid + 1])
+    lower.append(coupling[mid + 1] * scale)
+    below.append(source_low * scale)
+    middle = (source + lower[-1] * source_low) / (pivot + lower[-1] * pivot_low)
+    solved = [middle]
+    for k in range(mid - 1, -1, -1):
+        solved.insert(0, above[k] + upper[k] * solved[0])
+    for k in range(len(below) - 1, -1, -1):
+        solved.append(below[k] + lower[k] * solved[-1])
+    return solved
 
 
 def step_columns(temps, depth, surface, seawater):
@@ -47,27 +76,16 @@
     half = 0.5 * salt
     guess = temps
     for turn in range(SWEEPS):
-        if turn > 0:
-            guess = back_substitute(ratio, done)
         turned = [1.0 / g for g in guess]
         coupling = [base + salt * turned[0]]
         for k in range(1, VERTICAL_LEVELS):
             coupling.append(base + half * (turned[k - 1] + turned[k]))
         coupling.append(base + salt * turned[-1])
-        pivot = 1.0 + coupling[0]
-        source = temps[0] + coupling[0] * surface
-        ratio, done = [], []
-        for k in range(VERTICAL_LEVELS):
-            if k > 0:
-                pivot = 1.0 + ratio[k - 1] * pivot
-                source = temps[k] + ratio[k - 1] * source
-            scale = 1.0 / (pivot + coupling[k + 1])
-            if k < VERTICAL_LEVELS - 1:
-                ratio.append(coupling[k + 1] * scale)
-            else:
-                source = source + coupling[k + 1] * FREEZE_POINT
-            done.append(source * scale)
-    bottom = done[-1]
+        if turn < SWEEPS - 1:
+            guess = meet(temps, surface, coupling)
+    ratio, done, pivot, source = eliminate(temps, surface, coupling)
+    bottom = (source + coupling[-1] * FREEZE_POINT) / (pivot + coupling[-1])
+    done.append(bottom)
     thick = (
         depth
         + GROWTH_RATE * (BASE_CONDUCT + SALT_CONDUCT / bottom) * (FREEZE_POINT - bottom) * inverse
@@ -266,7 +284,6 @@
 
     arrive(held.at[pl.ds(0, FAST)], in_sem.at[last + 3])
     arrive(land_in, in_sem.at[last + 2])
-    arrive(blocks[0], in_sem.at[0])
     volume = held[area_at[0]] * held[depth_at[0]]
     coverage = held[area_at[0]]
     for c in range(1, DEPTH_CLASSES):
@@ -290,6 +307,7 @@
     for f in range(FIELDS):
         own[f] = fields[f]
 
+    arrive(blocks[0], in_sem.at[0])
     for c in range(0, 2):
         thermo(c)
     pl.semaphore_wait(barrier, devices - 1)

time: 11.8 us -> 11.8 us (level)
  no operation moved by 1% of the time
where the time goes in v3:
time: 11.8 us; the launch traced here: 11.6 us
  Pallas kernels  11 us (93%)
  between operations  0.64 us (5%)
    pallas_call x1, Pallas kernels, local(): pl.pallas_call(functools.partial(kernel, n_lat, n_lon), out_shape=[pltpu....  10.2 us
    pallas_call x1, Pallas kernels, local(): pl.pallas_call(put_out, out_shape=[jax.ShapeDtypeStruct(shape, f32) for s...  0.75 us

profile of v3, /device:TPU:0, one launch (start us, length us, event | category | flops | bytes accessed | tf_op | source)
XLA Modules:
  0.0 11.6 jit_solution(3006156356250905275)
XLA Ops:
  0.6 10.2 %ice_step.1 = (f32[35,16,128]{2,1,0:T(8,128)S(1)}, f32[5,16,128]{2,1,0:T(8,128)S(1)}, f32[2,16,128]{2,1,0:T(8,128)S(1)}, f32[3,16,128]{2,1,0:T(8,128)S(1)}, f32[1,4]{1,0:T(1,128)S(1)}) custom-call(f32[35,16,128]{2,1,0:T(8,128)} %bitcast.7, f32[5,16,128]{2,1,0:T(8,128)} %bitcast.8, f32[5,16,128]{2,1,0:T(8,128)} %bitcast.9, f32[16,128]{1,0:T(8,128)} %refs_3_.1, ...), custom_call_target="tpu_custom_call" | custom-call | tf_op jit(solution)/shard_map/ice_step/pallas_call | solution.py:448
  10.9 0.8 %put_out.1 = (f32[35,16,128]{2,1,0:T(8,128)}, f32[5,16,128]{2,1,0:T(8,128)}, f32[2,16,128]{2,1,0:T(8,128)}, f32[3,16,128]{2,1,0:T(8,128)}, f32[1,4]{1,0:T(1,128)}) custom-call(f32[35,16,128]{2,1,0:T(8,128)S(1)} %get-tuple-element.15.temp, f32[5,16,128]{2,1,0:T(8,128)S(1)} %get-tuple-element.16.thick, f32[2,16,128]{2,1,0:T(8,128)S(1)} %get-tuple-element.17.vel, ...), custom_call_target="tpu_custom_call" | custom-call | tf_op jit(solution)/shard_map/put_out/pallas_call | solution.py:470
